TPU v7x, 32 devices: a whole 2x2x4 slice. The times are simulated.
32 devices in a mesh: pa: 4 (over y, x), pb: 8 (over z, core).
Axes of the slice: x: 2, y: 2, z: 4, core: 2. Of those that a mesh axis runs over, the one named last changes fastest.
Arguments:
- right_side: float32 [32, 64, 128], P(None, 'pa', 'pb'), may hold values from -6 to 6
- coef_x: float32 [32, 64, 128], P(None, 'pa', 'pb'), may hold values from 0.1 to 4
- coef_y: float32 [32, 64, 128], P(None, 'pa', 'pb'), may hold values from 0.1 to 4
- coef_z: float32 [32, 64, 128], P(None, 'pa', 'pb'), may hold values from 0.1 to 4
Outputs:
- solution_field: float32 [32, 64, 128], P(None, 'pa', 'pb')
- residual: float32 [32, 64, 128], P(None, 'pa', 'pb')
All inputs are finite; a program needn't handle non-finite values.
Results may differ from a plain program's by a relative error of at most 0.0003.
Values sent between devices are 32-bit elements.
A program may use at most 64 MiB of HBM per device.

v0:
```python
import math

import jax
import jax.numpy as jnp
from jax import lax
from jax.sharding import PartitionSpec as P

ITERS = 4


mass_shift = 0.5
base_coef = 1.0


def padded_2(block, sides, width, periodic):
    for axis, dim in sides:
        count = lax.axis_size(axis)
        forward = [(i, i + 1) for i in range(count - 1)]
        if periodic:
            forward.append((count - 1, 0))
        backward = [(target, source) for source, target in forward]
        low = lax.ppermute(
            lax.slice_in_dim(block, block.shape[dim] - width, None, axis=dim), axis, forward
        )
        high = lax.ppermute(lax.slice_in_dim(block, 0, width, axis=dim), axis, backward)
        block = jnp.concatenate([low, block, high], axis=dim)
    return block


def shifted(x, axis, by):
    peers = lax.axis_size(axis)
    return lax.ppermute(x, axis, [(i, (i + by) % peers) for i in range(peers)])


def dft_tables(points):
    positions = lax.iota(jnp.int32, points)
    product = positions[:, None] * positions[None, :] % points
    angles = product.astype(jnp.float32) * (2.0 * math.pi / points)
    return (jnp.cos(angles), jnp.sin(angles))


def apply_along(matrix, values, target_dim):
    moved = jnp.tensordot(matrix, values, axes=([1], [target_dim]), precision=lax.Precision.HIGHEST)
    return jnp.moveaxis(moved, 0, target_dim)


def forward_complex(real_part, imag_part, target_dim):
    cosine_table, sine_table = dft_tables(real_part.shape[target_dim])
    new_real = apply_along(cosine_table, real_part, target_dim) + apply_along(
        sine_table, imag_part, target_dim
    )
    new_imag = apply_along(cosine_table, imag_part, target_dim) - apply_along(
        sine_table, real_part, target_dim
    )
    return (new_real, new_imag)


def inverse_complex(real_part, imag_part, target_dim):
    points = real_part.shape[target_dim]
    cosine_table, sine_table = dft_tables(points)
    inverse_scale = 1.0 / points
    new_real = (
        apply_along(cosine_table, real_part, target_dim)
        - apply_along(sine_table, imag_part, target_dim)
    ) * inverse_scale
    new_imag = (
        apply_along(cosine_table, imag_part, target_dim)
        + apply_along(sine_table, real_part, target_dim)
    ) * inverse_scale
    return (new_real, new_imag)


def wave_term(positions, points):
    return 2.0 - 2.0 * jnp.cos(2.0 * math.pi * positions.astype(jnp.float32) / points)


def divide_symbol(real_part, imag_part, starts, totals):
    wave_x = wave_term(starts[0] + lax.iota(jnp.int32, real_part.shape[0]), totals[0])
    wave_y = wave_term(starts[1] + lax.iota(jnp.int32, real_part.shape[1]), totals[1])
    wave_z = wave_term(starts[2] + lax.iota(jnp.int32, real_part.shape[2]), totals[2])
    symbol = mass_shift + base_coef * (
        wave_x[:, None, None] + wave_y[None, :, None] + wave_z[None, None, :]
    )
    return (real_part / symbol, imag_part / symbol)


def precondition(residual):
    count_x, rows_y, rows_z = residual.shape
    groups_a = lax.axis_size("pa")
    groups_b = lax.axis_size("pb")
    total_y = rows_y * groups_a
    total_z = rows_z * groups_b
    cosine_table, sine_table = dft_tables(count_x)
    real_part = apply_along(cosine_table, residual, 0)
    imag_part = -apply_along(sine_table, residual, 0)
    devices = groups_a * groups_b
    planes = count_x // devices

    def to_slab(values):
        arranged = values.reshape(groups_a, groups_b, planes, rows_y, rows_z)
        return arranged.transpose(2, 0, 3, 1, 4).reshape(planes, total_y, total_z)

    def from_slab(values):
        arranged = values.reshape(planes, groups_a, rows_y, groups_b, rows_z)
        return arranged.transpose(1, 3, 0, 2, 4).reshape(devices, planes, rows_y, rows_z)

    stacked_real = real_part.reshape(devices, planes, rows_y, rows_z)
    stacked_imag = imag_part.reshape(devices, planes, rows_y, rows_z)
    stacked_real, stacked_imag = (
        lax.all_to_all(stacked_real, ("pa", "pb"), split_axis=0, concat_axis=0, tiled=True),
        lax.all_to_all(stacked_imag, ("pa", "pb"), split_axis=0, concat_axis=0, tiled=True),
    )
    real_part = to_slab(stacked_real)
    imag_part = to_slab(stacked_imag)
    real_part, imag_part = forward_complex(real_part, imag_part, 1)
    real_part, imag_part = forward_complex(real_part, imag_part, 2)
    starts = (lax.axis_index(("pa", "pb")) * planes, 0, 0)
    real_part, imag_part = divide_symbol(real_part, imag_part, starts, (count_x, total_y, total_z))
    real_part, imag_part = inverse_complex(real_part, imag_part, 2)
    real_part, imag_part = inverse_complex(real_part, imag_part, 1)
    stacked_real, stacked_imag = (
        lax.all_to_all(from_slab(real_part), ("pa", "pb"), split_axis=0, concat_axis=0, tiled=True),
        lax.all_to_all(from_slab(imag_part), ("pa", "pb"), split_axis=0, concat_axis=0, tiled=True),
    )
    real_part = stacked_real.reshape(count_x, rows_y, rows_z)
    imag_part = stacked_imag.reshape(count_x, rows_y, rows_z)
    result = apply_along(cosine_table, real_part, 0) - apply_along(sine_table, imag_part, 0)
    return result * (1.0 / count_x)


def operate(grid_field, coefs, lower_coefs):
    padded = padded_2(grid_field, (("pa", 1), ("pb", 2)), 1, True)
    result = mass_shift * grid_field
    result = (
        result
        + coefs[0] * (grid_field - jnp.roll(grid_field, -1, 0))
        + lower_coefs[0] * (grid_field - jnp.roll(grid_field, 1, 0))
    )
    result = (
        result
        + coefs[1] * (grid_field - padded[:, 2:, 1:-1])
        + lower_coefs[1] * (grid_field - padded[:, :-2, 1:-1])
    )
    result = (
        result
        + coefs[2] * (grid_field - padded[:, 1:-1, 2:])
        + lower_coefs[2] * (grid_field - padded[:, 1:-1, :-2])
    )
    return result


def fit_sum(residual, precond):
    return lax.psum(jnp.sum(residual * precond), ("pa", "pb"))


def on_device(right_side, coef_x, coef_y, coef_z):
    edge_y = shifted(coef_y[:, -1:, :], "pa", 1)
    edge_z = shifted(coef_z[:, :, -1:], "pb", 1)
    lower_x = jnp.roll(coef_x, 1, 0)
    lower_y = jnp.concatenate([edge_y, coef_y[:, :-1, :]], axis=1)
    lower_z = jnp.concatenate([edge_z, coef_z[:, :, :-1]], axis=2)
    coefs = (coef_x, coef_y, coef_z)
    lower_coefs = (lower_x, lower_y, lower_z)
    solution_field = jnp.zeros_like(right_side)
    residual = right_side
    precond = precondition(residual)
    direction = precond
    fit_now = fit_sum(residual, precond)
    for iteration in range(ITERS):
        image_field = operate(direction, coefs, lower_coefs)
        step_size = fit_now / lax.psum(jnp.sum(direction * image_field), ("pa", "pb"))
        solution_field = solution_field + step_size * direction
        residual = residual - step_size * image_field
        if iteration + 1 < ITERS:
            precond = precondition(residual)
            fit_next = fit_sum(residual, precond)
            direction = precond + fit_next / fit_now * direction
            fit_now = fit_next
    return (solution_field, residual)


def solution(mesh):
    placed = (P(None, "pa", "pb"), P(None, "pa", "pb"), P(None, "pa", "pb"), P(None, "pa", "pb"))
    return jax.shard_map(
        on_device,
        mesh=mesh,
        in_specs=placed,
        out_specs=(P(None, "pa", "pb"), P(None, "pa", "pb")),
        check_vma=False,
    )
```

profile of v0, /device:TPU:0, one launch (start us, length us, event | category | flops | bytes accessed | tf_op | source)
XLA Modules:
  0.0 546.4 jit_solution(17384994631856300854)
XLA Ops:
  2.7 2.5 collective-permute-start.1
  7.4 4.9 all-to-all-start
  14.9 4.7 all-to-all-done
  19.6 2.6 all-to-all-start.1
  24.2 5.3 all-to-all-done.1
  37.3 2.6 all-to-all-start.2
  41.1 6.0 %all-to-all-done.2 = f32[32,1,256]{2,1,0:T(1,128)S(1)} async-done(((f32[32,1,256]{2,1,0:T(1,128)}), f32[32,1,256]{2,1,0:T(1,128)S(1)}, u32[]{:S(2)}, u32[]{:S(2)}) %all-to-all-start.2) | async-done | bytes 32800 | tf_op jit(solution)/shard_map/all_to_all | solution.py:122
  47.2 2.6 all-to-all-start.3
  51.1 5.9 %all-to-all-done.3 = f32[32,1,256]{2,1,0:T(1,128)S(1)} async-done(((f32[32,1,256]{2,1,0:T(1,128)}), f32[32,1,256]{2,1,0:T(1,128)S(1)}, u32[]{:S(2)}, u32[]{:S(2)}) %all-to-all-start.3) | async-done | bytes 32800 | tf_op jit(solution)/shard_map/all_to_all | solution.py:123
  59.1 2.3 collective-permute-start
  64.5 3.6 collective-permute-done.5
  69.0 38.5 %all-reduce = (f32[]{:T(128)}, f32[]{:T(128)}) all-reduce(f32[]{:T(128)} %get-tuple-element.3, f32[]{:T(128)} %get-tuple-element.2), channel_id=1, replica_groups=mesh['pa'=4,'pb'=8] {'pa','pb'}, use_global_device_ids=true, to_apply=%region_1.2 | all-reduce | flops 2 | bytes 16 | tf_op jit(solution)/shard_map/psum | solution.py:153
  110.5 5.5 %all-to-all-start.4 = ((f32[32,1,256]{2,1,0:T(1,128)}), f32[32,1,256]{2,1,0:T(1,128)S(1)}, u32[]{:S(2)}, u32[]{:S(2)}) async-start(f32[32,1,256]{2,1,0:T(1,128)} %reshape.622), calls=%async_computation.4 | async-start | bytes 65536 | tf_op jit(solution)/shard_map/all_to_all | solution.py:110
  116.9 6.3 %all-to-all-done.4 = f32[32,1,256]{2,1,0:T(1,128)S(1)} async-done(((f32[32,1,256]{2,1,0:T(1,128)}), f32[32,1,256]{2,1,0:T(1,128)S(1)}, u32[]{:S(2)}, u32[]{:S(2)}) %all-to-all-start.4) | async-done | bytes 32800 | tf_op jit(solution)/shard_map/all_to_all | solution.py:110
  123.2 2.6 all-to-all-start.5
  127.2 5.9 %all-to-all-done.5 = f32[32,1,256]{2,1,0:T(1,128)S(1)} async-done(((f32[32,1,256]{2,1,0:T(1,128)}), f32[32,1,256]{2,1,0:T(1,128)S(1)}, u32[]{:S(2)}, u32[]{:S(2)}) %all-to-all-start.5) | async-done | bytes 32800 | tf_op jit(solution)/shard_map/all_to_all | solution.py:111
  140.9 2.6 all-to-all-start.6
  144.8 6.0 %all-to-all-done.6 = f32[32,1,256]{2,1,0:T(1,128)S(1)} async-done(((f32[32,1,256]{2,1,0:T(1,128)}), f32[32,1,256]{2,1,0:T(1,128)S(1)}, u32[]{:S(2)}, u32[]{:S(2)}) %all-to-all-start.6) | async-done | bytes 32800 | tf_op jit(solution)/shard_map/all_to_all | solution.py:122
  150.8 2.6 all-to-all-start.7
  154.8 5.9 %all-to-all-done.7 = f32[32,1,256]{2,1,0:T(1,128)S(1)} async-done(((f32[32,1,256]{2,1,0:T(1,128)}), f32[32,1,256]{2,1,0:T(1,128)S(1)}, u32[]{:S(2)}, u32[]{:S(2)}) %all-to-all-start.7) | async-done | bytes 32800 | tf_op jit(solution)/shard_map/all_to_all | solution.py:123
  162.7 38.3 %psum.58 = f32[]{:T(128)} all-reduce(f32[]{:T(128)} %multiply_reduce_fusion.5), channel_id=1, replica_groups=mesh['pa'=4,'pb'=8] {'pa','pb'}, use_global_device_ids=true, to_apply=%region_5.6 | all-reduce | flops 1 | bytes 8 | tf_op jit(solution)/shard_map/psum | solution.py:153
  202.3 2.3 collective-permute-start.7
  209.8 3.6 collective-permute-done.9
  214.1 38.3 %psum.59 = f32[]{:T(128)} all-reduce(f32[]{:T(128)} %get-tuple-element.10), channel_id=1, replica_groups=mesh['pa'=4,'pb'=8] {'pa','pb'}, use_global_device_ids=true, to_apply=%region_7.8 | all-reduce | flops 1 | bytes 8 | tf_op jit(solution)/shard_map/psum | solution.py:171
  255.3 5.9 %all-to-all-start.8 = ((f32[32,1,256]{2,1,0:T(1,128)}), f32[32,1,256]{2,1,0:T(1,128)S(1)}, u32[]{:S(2)}, u32[]{:S(2)}) async-start(f32[32,1,256]{2,1,0:T(1,128)} %reshape.630), calls=%async_computation.8 | async-start | bytes 65536 | tf_op jit(solution)/shard_map/all_to_all | solution.py:110
  262.2 6.3 %all-to-all-done.8 = f32[32,1,256]{2,1,0:T(1,128)S(1)} async-done(((f32[32,1,256]{2,1,0:T(1,128)}), f32[32,1,256]{2,1,0:T(1,128)S(1)}, u32[]{:S(2)}, u32[]{:S(2)}) %all-to-all-start.8) | async-done | bytes 32800 | tf_op jit(solution)/shard_map/all_to_all | solution.py:110
  268.6 2.8 all-to-all-start.9
  272.8 5.9 %all-to-all-done.9 = f32[32,1,256]{2,1,0:T(1,128)S(1)} async-done(((f32[32,1,256]{2,1,0:T(1,128)}), f32[32,1,256]{2,1,0:T(1,128)S(1)}, u32[]{:S(2)}, u32[]{:S(2)}) %all-to-all-start.9) | async-done | bytes 32800 | tf_op jit(solution)/shard_map/all_to_all | solution.py:111
  286.5 2.6 all-to-all-start.10
  290.3 6.0 %all-to-all-done.10 = f32[32,1,256]{2,1,0:T(1,128)S(1)} async-done(((f32[32,1,256]{2,1,0:T(1,128)}), f32[32,1,256]{2,1,0:T(1,128)S(1)}, u32[]{:S(2)}, u32[]{:S(2)}) %all-to-all-start.10) | async-done | bytes 32800 | tf_op jit(solution)/shard_map/all_to_all | solution.py:122
  296.3 2.6 all-to-all-start.11
  300.3 5.9 %all-to-all-done.11 = f32[32,1,256]{2,1,0:T(1,128)S(1)} async-done(((f32[32,1,256]{2,1,0:T(1,128)}), f32[32,1,256]{2,1,0:T(1,128)S(1)}, u32[]{:S(2)}, u32[]{:S(2)}) %all-to-all-start.11) | async-done | bytes 32800 | tf_op jit(solution)/shard_map/all_to_all | solution.py:123
  308.2 38.3 %psum.60 = f32[]{:T(128)} all-reduce(f32[]{:T(128)} %multiply_reduce_fusion.3), channel_id=1, replica_groups=mesh['pa'=4,'pb'=8] {'pa','pb'}, use_global_device_ids=true, to_apply=%region_9.10 | all-reduce | flops 1 | bytes 8 | tf_op jit(solution)/shard_map/psum | solution.py:153
  347.9 2.3 collective-permute-start.11
  355.3 3.6 collective-permute-done.13
  359.7 38.3 %psum.61 = f32[]{:T(128)} all-reduce(f32[]{:T(128)} %get-tuple-element.8), channel_id=1, replica_groups=mesh['pa'=4,'pb'=8] {'pa','pb'}, use_global_device_ids=true, to_apply=%region_11.12 | all-reduce | flops 1 | bytes 8 | tf_op jit(solution)/shard_map/psum | solution.py:171
  401.0 5.9 %all-to-all-start.12 = ((f32[32,1,256]{2,1,0:T(1,128)}), f32[32,1,256]{2,1,0:T(1,128)S(1)}, u32[]{:S(2)}, u32[]{:S(2)}) async-start(f32[32,1,256]{2,1,0:T(1,128)} %reshape.638), calls=%async_computation.12 | async-start | bytes 65536 | tf_op jit(solution)/shard_map/all_to_all | solution.py:110
  407.9 6.3 %all-to-all-done.12 = f32[32,1,256]{2,1,0:T(1,128)S(1)} async-done(((f32[32,1,256]{2,1,0:T(1,128)}), f32[32,1,256]{2,1,0:T(1,128)S(1)}, u32[]{:S(2)}, u32[]{:S(2)}) %all-to-all-start.12) | async-done | bytes 32800 | tf_op jit(solution)/shard_map/all_to_all | solution.py:110
  414.2 2.8 all-to-all-start.13
  418.5 5.9 %all-to-all-done.13 = f32[32,1,256]{2,1,0:T(1,128)S(1)} async-done(((f32[32,1,256]{2,1,0:T(1,128)}), f32[32,1,256]{2,1,0:T(1,128)S(1)}, u32[]{:S(2)}, u32[]{:S(2)}) %all-to-all-start.13) | async-done | bytes 32800 | tf_op jit(solution)/shard_map/all_to_all | solution.py:111
  432.2 2.6 all-to-all-start.14
  436.0 6.0 %all-to-all-done.14 = f32[32,1,256]{2,1,0:T(1,128)S(1)} async-done(((f32[32,1,256]{2,1,0:T(1,128)}), f32[32,1,256]{2,1,0:T(1,128)S(1)}, u32[]{:S(2)}, u32[]{:S(2)}) %all-to-all-start.14) | async-done | bytes 32800 | tf_op jit(solution)/shard_map/all_to_all | solution.py:122
  442.0 2.6 all-to-all-start.15
  446.0 5.9 %all-to-all-done.15 = f32[32,1,256]{2,1,0:T(1,128)S(1)} async-done(((f32[32,1,256]{2,1,0:T(1,128)}), f32[32,1,256]{2,1,0:T(1,128)S(1)}, u32[]{:S(2)}, u32[]{:S(2)}) %all-to-all-start.15) | async-done | bytes 32800 | tf_op jit(solution)/shard_map/all_to_all | solution.py:123
  453.9 38.3 %psum.62 = f32[]{:T(128)} all-reduce(f32[]{:T(128)} %multiply_reduce_fusion.1), channel_id=1, replica_groups=mesh['pa'=4,'pb'=8] {'pa','pb'}, use_global_device_ids=true, to_apply=%region_13.14 | all-reduce | flops 1 | bytes 8 | tf_op jit(solution)/shard_map/psum | solution.py:153
  493.7 2.3 collective-permute-start.15
  501.1 3.6 collective-permute-done.17
  505.5 38.3 %psum.63 = f32[]{:T(128)} all-reduce(f32[]{:T(128)} %get-tuple-element.6), channel_id=1, replica_groups=mesh['pa'=4,'pb'=8] {'pa','pb'}, use_global_device_ids=true, to_apply=%region_15.16 | all-reduce | flops 1 | bytes 8 | tf_op jit(solution)/shard_map/psum | solution.py:171
  (253 shorter events, 92.3 us)
Async XLA Ops:
  1.5 62.3 %collective-permute-start.4 = (f32[32,16,1]{0,2,1:T(1,128)S(1)}, f32[32,16,1]{0,2,1:T(1,128)S(1)}, u32[]{:S(2)}, u32[]{:S(2)}) collective-permute-start(f32[32,16,1]{0,2,1:T(1,128)S(1)} %slice.196), channel_id=1, source_target_pairs={{0,1},{1,2},{2,3},{3,4},{4,5},{5,6},{6,7},{7,0},{8,9},{9,10},{10,1... | collective-permute-start | bytes 6152 | tf_op jit(solution)/shard_map/ppermute | solution.py:32
  2.7 61.1 %collective-permute-start.1 = (f32[32,1,16]{0,2,1:T(8,128)S(1)}, f32[32,1,16]{0,2,1:T(8,128)S(1)}, u32[]{:S(2)}, u32[]{:S(2)}) collective-permute-start(f32[32,1,16]{0,2,1:T(8,128)S(1)} %slice.190), channel_id=1, source_target_pairs={{0,8},{8,16},{16,24},{24,0},{1,9},{9,17},{17,25},{25,1},{2,10},{10... | collective-permute-start | bytes 6152 | tf_op jit(solution)/shard_map/ppermute | solution.py:32
  6.6 5.8 %copy-start.2 = (f32[32,16,16]{0,2,1:T(8,128)S(1)}, f32[32,16,16]{0,2,1:T(8,128)}, u32[]{:S(2)}) copy-start(f32[32,16,16]{0,2,1:T(8,128)} %param.6) | copy-start | bytes 98308
  7.4 12.2 %all-to-all-start = ((f32[32,1,256]{2,1,0:T(1,128)}), f32[32,1,256]{2,1,0:T(1,128)S(1)}, u32[]{:S(2)}, u32[]{:S(2)}) async-start(f32[32,1,256]{2,1,0:T(1,128)} %reshape.614), calls=%async_computation | async-start | bytes 65536 | tf_op jit(solution)/shard_map/all_to_all | solution.py:110
  12.3 0.9 copy-start.3
  13.8 0.9 copy-start.1
  19.6 9.9 %all-to-all-start.1 = ((f32[32,1,256]{2,1,0:T(1,128)}), f32[32,1,256]{2,1,0:T(1,128)S(1)}, u32[]{:S(2)}, u32[]{:S(2)}) async-start(f32[32,1,256]{2,1,0:T(1,128)} %reshape.616), calls=%async_computation.1 | async-start | bytes 65536 | tf_op jit(solution)/shard_map/all_to_all | solution.py:111
  37.3 9.9 %all-to-all-start.2 = ((f32[32,1,256]{2,1,0:T(1,128)}), f32[32,1,256]{2,1,0:T(1,128)S(1)}, u32[]{:S(2)}, u32[]{:S(2)}) async-start(f32[32,1,256]{2,1,0:T(1,128)} %reshape.618), calls=%async_computation.2 | async-start | bytes 65536 | tf_op jit(solution)/shard_map/all_to_all | solution.py:122
  47.2 9.9 %all-to-all-start.3 = ((f32[32,1,256]{2,1,0:T(1,128)}), f32[32,1,256]{2,1,0:T(1,128)S(1)}, u32[]{:S(2)}, u32[]{:S(2)}) async-start(f32[32,1,256]{2,1,0:T(1,128)} %reshape.620), calls=%async_computation.3 | async-start | bytes 65536 | tf_op jit(solution)/shard_map/all_to_all | solution.py:123
  58.5 4.6 collective-permute-start.2
  59.1 3.9 collective-permute-start
  63.1 1.4 collective-permute-start.3
  63.1 5.0 copy-start
  63.2 4.9 collective-permute-start.5
  110.5 12.8 %all-to-all-start.4 = ((f32[32,1,256]{2,1,0:T(1,128)}), f32[32,1,256]{2,1,0:T(1,128)S(1)}, u32[]{:S(2)}, u32[]{:S(2)}) async-start(f32[32,1,256]{2,1,0:T(1,128)} %reshape.622), calls=%async_computation.4 | async-start | bytes 65536 | tf_op jit(solution)/shard_map/all_to_all | solution.py:110
  123.2 9.9 %all-to-all-start.5 = ((f32[32,1,256]{2,1,0:T(1,128)}), f32[32,1,256]{2,1,0:T(1,128)S(1)}, u32[]{:S(2)}, u32[]{:S(2)}) async-start(f32[32,1,256]{2,1,0:T(1,128)} %reshape.624), calls=%async_computation.5 | async-start | bytes 65536 | tf_op jit(solution)/shard_map/all_to_all | solution.py:111
  140.9 9.9 %all-to-all-start.6 = ((f32[32,1,256]{2,1,0:T(1,128)}), f32[32,1,256]{2,1,0:T(1,128)S(1)}, u32[]{:S(2)}, u32[]{:S(2)}) async-start(f32[32,1,256]{2,1,0:T(1,128)} %reshape.626), calls=%async_computation.6 | async-start | bytes 65536 | tf_op jit(solution)/shard_map/all_to_all | solution.py:122
  150.8 9.9 %all-to-all-start.7 = ((f32[32,1,256]{2,1,0:T(1,128)}), f32[32,1,256]{2,1,0:T(1,128)S(1)}, u32[]{:S(2)}, u32[]{:S(2)}) async-start(f32[32,1,256]{2,1,0:T(1,128)} %reshape.628), calls=%async_computation.7 | async-start | bytes 65536 | tf_op jit(solution)/shard_map/all_to_all | solution.py:123
  202.3 4.6 collective-permute-start.7
  204.6 3.7 collective-permute-start.6
  208.3 1.4 collective-permute-start.8
  208.4 4.9 collective-permute-start.9
  255.3 13.2 %all-to-all-start.8 = ((f32[32,1,256]{2,1,0:T(1,128)}), f32[32,1,256]{2,1,0:T(1,128)S(1)}, u32[]{:S(2)}, u32[]{:S(2)}) async-start(f32[32,1,256]{2,1,0:T(1,128)} %reshape.630), calls=%async_computation.8 | async-start | bytes 65536 | tf_op jit(solution)/shard_map/all_to_all | solution.py:110
  268.6 10.1 %all-to-all-start.9 = ((f32[32,1,256]{2,1,0:T(1,128)}), f32[32,1,256]{2,1,0:T(1,128)S(1)}, u32[]{:S(2)}, u32[]{:S(2)}) async-start(f32[32,1,256]{2,1,0:T(1,128)} %reshape.632), calls=%async_computation.9 | async-start | bytes 65536 | tf_op jit(solution)/shard_map/all_to_all | solution.py:111
  286.5 9.9 %all-to-all-start.10 = ((f32[32,1,256]{2,1,0:T(1,128)}), f32[32,1,256]{2,1,0:T(1,128)S(1)}, u32[]{:S(2)}, u32[]{:S(2)}) async-start(f32[32,1,256]{2,1,0:T(1,128)} %reshape.634), calls=%async_computation.10 | async-start | bytes 65536 | tf_op jit(solution)/shard_map/all_to_all | solution.py:122
  296.3 9.9 %all-to-all-start.11 = ((f32[32,1,256]{2,1,0:T(1,128)}), f32[32,1,256]{2,1,0:T(1,128)S(1)}, u32[]{:S(2)}, u32[]{:S(2)}) async-start(f32[32,1,256]{2,1,0:T(1,128)} %reshape.636), calls=%async_computation.11 | async-start | bytes 65536 | tf_op jit(solution)/shard_map/all_to_all | solution.py:123
  347.9 4.6 collective-permute-start.11
  350.2 3.7 collective-permute-start.10
  353.9 1.4 collective-permute-start.12
  353.9 4.9 collective-permute-start.13
  401.0 13.2 %all-to-all-start.12 = ((f32[32,1,256]{2,1,0:T(1,128)}), f32[32,1,256]{2,1,0:T(1,128)S(1)}, u32[]{:S(2)}, u32[]{:S(2)}) async-start(f32[32,1,256]{2,1,0:T(1,128)} %reshape.638), calls=%async_computation.12 | async-start | bytes 65536 | tf_op jit(solution)/shard_map/all_to_all | solution.py:110
  414.2 10.1 %all-to-all-start.13 = ((f32[32,1,256]{2,1,0:T(1,128)}), f32[32,1,256]{2,1,0:T(1,128)S(1)}, u32[]{:S(2)}, u32[]{:S(2)}) async-start(f32[32,1,256]{2,1,0:T(1,128)} %reshape.640), calls=%async_computation.13 | async-start | bytes 65536 | tf_op jit(solution)/shard_map/all_to_all | solution.py:111
  432.2 9.9 %all-to-all-start.14 = ((f32[32,1,256]{2,1,0:T(1,128)}), f32[32,1,256]{2,1,0:T(1,128)S(1)}, u32[]{:S(2)}, u32[]{:S(2)}) async-start(f32[32,1,256]{2,1,0:T(1,128)} %reshape.642), calls=%async_computation.14 | async-start | bytes 65536 | tf_op jit(solution)/shard_map/all_to_all | solution.py:122
  442.0 9.9 %all-to-all-start.15 = ((f32[32,1,256]{2,1,0:T(1,128)}), f32[32,1,256]{2,1,0:T(1,128)S(1)}, u32[]{:S(2)}, u32[]{:S(2)}) async-start(f32[32,1,256]{2,1,0:T(1,128)} %reshape.644), calls=%async_computation.15 | async-start | bytes 65536 | tf_op jit(solution)/shard_map/all_to_all | solution.py:123
  493.7 4.6 collective-permute-start.15
  496.0 3.7 collective-permute-start.14
  499.7 1.4 collective-permute-start.16
  499.7 4.9 collective-permute-start.17
where the time goes:
time: 557 us; the launch traced here: 546 us
  blocking collectives  268 us (48%)
  waiting for transfers between devices  122 us (22%)
  starting transfers between devices  70.7 us (13%)
  matrix products  31.1 us (6%)
  local copies, waits for them, and re-layouts  23.8 us (4%)
  other arithmetic  18.7 us (3%)
  between operations  11.9 us (2%)
    psum x4, blocking collectives, fit_sum(): return lax.psum(jnp.sum(residual * precond), ('pa', 'pb'))  154 us
    psum x3, blocking collectives, on_device(): lax.psum(jnp.sum(direction * image_field), ('pa', 'pb'))  115 us
    dot_general x64, matrix products, apply_along(): jnp.tensordot(matrix, values, axes=([1], [target_dim]), precision=lax.Pre...  24.8 us
    all_to_all x4, waiting for transfers between devices, precondition(): lax.all_to_all(from_slab(real_part), ('pa', 'pb'), split_axis=0, concat_a...  24.1 us
    all_to_all x4, waiting for transfers between devices, precondition(): lax.all_to_all(stacked_real, ('pa', 'pb'), split_axis=0, concat_axis=0, t...  23.7 us
    all_to_all x4, waiting for transfers between devices, precondition(): lax.all_to_all(from_slab(imag_part), ('pa', 'pb'), split_axis=0, concat_a...  23.5 us
    all_to_all x4, waiting for transfers between devices, precondition(): lax.all_to_all(stacked_imag, ('pa', 'pb'), split_axis=0, concat_axis=0, t...  22.8 us
    all_to_all x4, starting transfers between devices, precondition(): lax.all_to_all(stacked_real, ('pa', 'pb'), split_axis=0, concat_axis=0, t...  22.3 us
  transfers between devices with their start and end apart: 34, of which 31 were waited for; matrix products, arithmetic and copies ran while one was open for 6% of the time, Pallas kernels for 0%

commit v1 on v0

v1 whole, which is shorter than its diff:
```python
import functools
import math

import jax
import jax.numpy as jnp
import numpy as np
from jax import lax
from jax.experimental import pallas as pl
from jax.experimental.pallas import tpu as pltpu
from jax.sharding import PartitionSpec as P

ITERS = 4
MESH = pl.DeviceIdType.MESH
LANES = 128
mass_shift = 0.5
base_coef = 1.0


def real_basis(points):
    position = np.arange(points)[:, None]
    mode = np.arange(points)[None, :]
    wave = (mode + 1) // 2
    angle = 2.0 * np.pi * ((position * wave) % points) / points
    basis = np.where(mode % 2 == 1, np.cos(angle), np.sin(angle)) * math.sqrt(2.0 / points)
    basis[:, 0] = 1.0 / math.sqrt(points)
    if points % 2 == 0:
        basis[:, -1] = np.cos(np.pi * np.arange(points)) / math.sqrt(points)
    return basis, 2.0 - 2.0 * np.cos(2.0 * np.pi * wave[0] / points)


def halves(matrix):
    high = matrix.astype(np.float32).astype(jnp.bfloat16)
    low = (matrix - high.astype(np.float64)).astype(np.float32).astype(jnp.bfloat16)
    return high, low


def left_table(matrix):
    high, low = halves(matrix)
    return np.concatenate([high, high, low], axis=1)


def right_table(matrix):
    high, low = halves(matrix)
    return np.concatenate([high, high, low], axis=0)


def split(values, axis):
    high = values.astype(jnp.bfloat16)
    low = (values - high.astype(jnp.float32)).astype(jnp.bfloat16)
    return jnp.concatenate([high, low, high], axis=axis)


def left_mul(table, values):
    return jnp.dot(table[...], split(values, 0), preferred_element_type=jnp.float32)


def right_mul(values, table):
    return jnp.dot(split(values, 1), table[...], preferred_element_type=jnp.float32)


def lane_roll(values, by):
    return pltpu.roll(values, by % values.shape[-1], values.ndim - 1)


def row_roll(values, by):
    return pltpu.roll(values, by % values.shape[-2], values.ndim - 2)


def swap_blocks(tile, width):
    row = lax.broadcasted_iota(jnp.int32, tile.shape, 0)
    block = lax.broadcasted_iota(jnp.int32, tile.shape, 1) // width
    for bit in (1, 2, 4):
        row_set = (row // bit) % 2 == 1
        block_set = (block // bit) % 2 == 1
        upper = lane_roll(row_roll(tile, bit), -bit * width)
        lower = lane_roll(row_roll(tile, -bit), bit * width)
        tile = jnp.where(row_set == block_set, tile, jnp.where(row_set, upper, lower))
    return tile


def kernel(
    na, nb, dims,
    right_ref, cx_ref, cy_ref, cz_ref,
    x_fwd, x_inv, y_fwd, y_inv, z_fwd, z_inv, wave_x_ref, wave_yz_ref,
    sol_ref, res_ref,
    send_f, recv_f, send_b, recv_b, send_d, recv_d, edge_y, edge_z,
    send_sem, recv_sem, edge_send, edge_recv, own_sem,
):
    nx, ry, rz = dims
    n = na * nb
    group = LANES // rz
    my_a, my_b = lax.axis_index("pa"), lax.axis_index("pb")
    me = my_a * nb + my_b

    barrier = pltpu.get_barrier_semaphore()

    def greet(step, carry):
        peer = lax.rem(me + step, n)
        pl.semaphore_signal(
            barrier, inc=1, device_id=(peer // nb, lax.rem(peer, nb)), device_id_type=MESH
        )
        return carry

    lax.fori_loop(1, n, greet, 0)
    pl.semaphore_wait(barrier, n - 1)

    def exchange(src, dst, rows, phase, by_peer):
        def own(base):
            return src.at[pl.ds(base, rows), :]

        def send(step, carry):
            peer = lax.rem(me + step, n)
            source = src.at[pl.ds(peer * rows, rows), :] if by_peer else src.at[pl.ds(0, rows), :]
            pltpu.make_async_remote_copy(
                src_ref=source,
                dst_ref=dst.at[pl.ds(me * rows, rows), :],
                send_sem=send_sem.at[phase],
                recv_sem=recv_sem.at[phase],
                device_id=(peer // nb, lax.rem(peer, nb)),
                device_id_type=MESH,
            ).start()
            return carry

        lax.fori_loop(1, n, send, 0, unroll=n <= 32)
        source = src[pl.ds(me * rows, rows), :] if by_peer else src[pl.ds(0, rows), :]
        dst[pl.ds(me * rows, rows), :] = source

    def arrive(dst, rows, phase):
        every = dst.at[pl.ds(0, (n - 1) * rows), :]
        pltpu.make_async_copy(every, every, recv_sem.at[phase]).wait()

    def drain(dst, rows, phase):
        every = dst.at[pl.ds(0, (n - 1) * rows), :]
        pltpu.make_async_copy(every, every, send_sem.at[phase]).wait()

    lane = lax.broadcasted_iota(jnp.int32, (nx, LANES), 1)
    z_at, y_at = lane % rz, lane // rz
    z_first, z_last = z_at == 0, z_at == rz - 1
    y_first, y_last = y_at == 0, y_at == group - 1

    def parts(ref):
        return ref[:, :LANES], ref[:, LANES:]

    def forward(first, second, partial, phase):
        modes = left_mul(x_fwd, jnp.concatenate([first, second], axis=1))
        out = send_f.at[phase]
        out[pl.ds(0, nx, stride=3), :] = modes[:, :LANES]
        out[pl.ds(1, nx, stride=3), :] = modes[:, LANES:]
        out[pl.ds(2, nx, stride=3), :] = jnp.broadcast_to(partial, (nx, LANES))
        exchange(out, recv_f.at[phase], 3, phase, True)

    def plane(phase):
        came = recv_f.at[phase]
        arrive(came, 3, phase)
        rows = []
        for a in range(na):
            for h in range(2):
                tiles = [
                    swap_blocks(came[pl.ds((a * nb + high * 8) * 3 + h, 8, stride=3), :], rz)
                    for high in range(nb // 8)
                ]
                rows.append(tiles[0] if len(tiles) == 1 else jnp.concatenate(tiles, axis=1))
        values = jnp.concatenate(rows, axis=0)
        total = jnp.sum(came[pl.ds(2, n, stride=3), :], keepdims=True)
        return left_mul(y_fwd, right_mul(values, z_fwd)), total

    tile_lane = lax.broadcasted_iota(jnp.int32, (nb, LANES), 1)
    tile_z, tile_y = tile_lane % rz, tile_lane // rz

    def backward(spectrum, partial, phase):
        values = right_mul(left_mul(y_inv, spectrum), z_inv)
        tiles = []
        for a in range(na):
            pair = []
            for h in range(2):
                at = (a * 2 + h) * 8
                cut = [
                    swap_blocks(values[at : at + 8, high * LANES : (high + 1) * LANES], rz)
                    for high in range(nb // 8)
                ]
                pair.append(cut[0] if len(cut) == 1 else jnp.concatenate(cut, axis=0))
            tiles.append(pair)
        out = send_b.at[phase]
        for a in range(na):
            t0, t1 = tiles[a]
            edges_z = jnp.where(
                tile_z == 0,
                row_roll(t0, -1),
                jnp.where(
                    tile_z == 1,
                    lane_roll(row_roll(t1, -1), 1),
                    jnp.where(
                        tile_z == rz - 1,
                        row_roll(t0, 1),
                        lane_roll(row_roll(t1, 1), -1),
                    ),
                ),
            )
            edges_y = jnp.where(
                tile_y == 0,
                tiles[(a + 1) % na][0],
                jnp.where(tile_y == group - 1, tiles[(a - 1) % na][1], partial),
            )
            for j, rows in enumerate((t0, t1, edges_z, edges_y)):
                out[pl.ds(a * nb * 4 + j, nb, stride=4), :] = rows
        exchange(out, recv_b.at[phase], 4, ITERS + phase, True)

    def block(phase):
        came = recv_b.at[phase]
        arrive(came, 4, ITERS + phase)
        pieces = [came[pl.ds(j, nx, stride=4), :] for j in range(4)]
        total = jnp.sum(jnp.where(lane == rz, pieces[3], 0.0), keepdims=True)
        values = left_mul(x_inv, jnp.concatenate(pieces, axis=1))
        return [values[:, j * LANES : (j + 1) * LANES] for j in range(4)], total

    zero_row = jnp.zeros((1, LANES), jnp.float32)
    right = parts(right_ref)
    forward(right[0], right[1], zero_row, 0)

    copies = (
        pltpu.make_async_remote_copy(
            src_ref=cy_ref.at[:, pl.ds(LANES, LANES)],
            dst_ref=edge_y,
            send_sem=edge_send.at[0],
            recv_sem=edge_recv.at[0],
            device_id=(lax.rem(my_a + 1, na), my_b),
            device_id_type=MESH,
        ),
        pltpu.make_async_remote_copy(
            src_ref=cz_ref,
            dst_ref=edge_z,
            send_sem=edge_send.at[1],
            recv_sem=edge_recv.at[1],
            device_id=(my_a, lax.rem(my_b + 1, nb)),
            device_id_type=MESH,
        ),
    )
    for copy in copies:
        copy.start()

    def operate(p, coefs):
        upper, lower = coefs
        edge_of_z, edge_of_y = p[2], p[3]
        above_y = (
            jnp.where(y_last, lane_roll(p[1], -rz), lane_roll(p[0], -rz)),
            jnp.where(y_last, lane_roll(edge_of_y, -rz), lane_roll(p[1], -rz)),
        )
        below_y = (
            jnp.where(y_first, lane_roll(edge_of_y, rz), lane_roll(p[0], rz)),
            jnp.where(y_first, lane_roll(p[0], rz), lane_roll(p[1], rz)),
        )
        result = []
        for h in range(2):
            own = p[h]
            above_z = jnp.where(z_last, lane_roll(edge_of_z, rz - 1 - h), lane_roll(own, -1))
            below_z = jnp.where(z_first, lane_roll(edge_of_z, h + 1 - rz), lane_roll(own, 1))
            total = mass_shift * own
            total = (
                total
                + upper[0][h] * (own - row_roll(own, -1))
                + lower[0][h] * (own - row_roll(own, 1))
            )
            total = total + upper[1][h] * (own - above_y[h]) + lower[1][h] * (own - below_y[h])
            total = total + upper[2][h] * (own - above_z) + lower[2][h] * (own - below_z)
            result.append(total)
        return result

    planes_row = wave_x_ref[pl.ds(me, 1), :1]
    inverse = 1.0 / (mass_shift + base_coef * (planes_row + wave_yz_ref[...]))

    spectrum = direction = coefs = fit_now = step_size = None
    solution_field, residual = None, right
    for iteration in range(ITERS):
        image_hat, inner = plane(iteration)
        if iteration == 0:
            spectrum = image_hat
        else:
            step_size = fit_now / inner
            spectrum = spectrum - step_size * image_hat
        scaled = spectrum * inverse
        backward(scaled, jnp.sum(spectrum * scaled, keepdims=True), iteration)
        if iteration == 0:
            for copy in copies:
                copy.wait()
            cx, cy, cz = parts(cx_ref), parts(cy_ref), parts(cz_ref)
            near_y, near_z = edge_y[...], parts(edge_z)
            lower_x = [row_roll(c, 1) for c in cx]
            lower_y = [
                jnp.where(y_first, lane_roll(near_y, rz), lane_roll(cy[0], rz)),
                jnp.where(y_first, lane_roll(cy[0], rz), lane_roll(cy[1], rz)),
            ]
            lower_z = [
                jnp.where(z_first, lane_roll(near_z[h], 1 - rz), lane_roll(cz[h], 1))
                for h in range(2)
            ]
            coefs = ((cx, cy, cz), (lower_x, lower_y, lower_z))
        else:
            residual = [r - step_size * i for r, i in zip(residual, image)]
            added = [step_size * d for d in direction[:2]]
            solution_field = (
                added if solution_field is None
                else [s + d for s, d in zip(solution_field, added)]
            )
        precond, fit_next = block(iteration)
        if iteration == 0:
            direction = precond
        else:
            ratio = fit_next / fit_now
            direction = [u + ratio * d for u, d in zip(precond, direction)]
        fit_now = fit_next
        image = operate(direction, coefs)
        partial = jnp.sum(direction[0] * image[0] + direction[1] * image[1], axis=0, keepdims=True)
        if iteration + 1 < ITERS:
            forward(image[0], image[1], partial, iteration + 1)

    send_d[...] = jnp.broadcast_to(partial, send_d.shape)
    exchange(send_d, recv_d, 1, 2 * ITERS, False)
    arrive(recv_d, 1, 2 * ITERS)
    step_size = fit_now / jnp.sum(recv_d[...], keepdims=True)
    for h in range(2):
        at = pl.ds(h * LANES, LANES)
        sol_ref[:, at] = solution_field[h] + step_size * direction[h]
        res_ref[:, at] = residual[h] - step_size * image[h]
    for phase in range(ITERS):
        drain(recv_f.at[phase], 3, phase)
        drain(recv_b.at[phase], 4, ITERS + phase)
    drain(recv_d, 1, 2 * ITERS)


def solution(mesh):
    na, nb = mesh.shape["pa"], mesh.shape["pb"]
    n = na * nb

    def on_device(right_side, coef_x, coef_y, coef_z):
        nx, ry, rz = right_side.shape
        cells = ry * rz
        assert nx == n and cells == 2 * LANES and LANES // rz == 8 and nb % 8 == 0
        basis_x, wave_x = real_basis(nx)
        basis_y, wave_y = real_basis(ry * na)
        basis_z, wave_z = real_basis(rz * nb)
        tables = (
            left_table(basis_x.T), left_table(basis_x),
            left_table(basis_y.T), left_table(basis_y),
            right_table(basis_z), right_table(basis_z.T),
            np.broadcast_to(wave_x[:, None], (nx, LANES)).astype(np.float32),
            (wave_y[:, None] + wave_z[None, :]).astype(np.float32),
        )
        flat = [v.reshape(nx, cells) for v in (right_side, coef_x, coef_y, coef_z)]
        shape = jax.ShapeDtypeStruct((nx, cells), jnp.float32)
        vmem = pl.BlockSpec(memory_space=pltpu.VMEM)
        f32 = jnp.float32
        outs = pl.pallas_call(
            functools.partial(kernel, na, nb, (nx, ry, rz)),
            out_shape=(shape, shape),
            in_specs=[vmem] * 12,
            out_specs=(vmem, vmem),
            scratch_shapes=[
                pltpu.VMEM((ITERS, n * 3, LANES), f32),
                pltpu.VMEM((ITERS, n * 3, LANES), f32),
                pltpu.VMEM((ITERS, n * 4, LANES), f32),
                pltpu.VMEM((ITERS, n * 4, LANES), f32),
                pltpu.VMEM((8, LANES), f32),
                pltpu.VMEM((n, LANES), f32),
                pltpu.VMEM((nx, LANES), f32),
                pltpu.VMEM((nx, cells), f32),
                pltpu.SemaphoreType.DMA((2 * ITERS + 1,)),
                pltpu.SemaphoreType.DMA((2 * ITERS + 1,)),
                pltpu.SemaphoreType.DMA((2,)),
                pltpu.SemaphoreType.DMA((2,)),
                pltpu.SemaphoreType.DMA,
            ],
            compiler_params=pltpu.CompilerParams(collective_id=0, has_side_effects=True),
        )(*flat, *[jnp.asarray(t) for t in tables])
        return tuple(o.reshape(nx, ry, rz) for o in outs)

    spec = P(None, "pa", "pb")
    return jax.shard_map(
        on_device, mesh=mesh, in_specs=(spec,) * 4, out_specs=(spec, spec), check_vma=False
    )
```

time: 557 us -> 61.7 us (0.11); the launches traced: 546 us -> 61.5 us
  blocking collectives: 268 us -> 0 us
  waiting for transfers between devices: 122 us -> 0 us
  starting transfers between devices: 70.7 us -> 0 us
  Pallas kernels: 0 us -> 54.8 us
  matrix products: 31.1 us -> 0 us
  other arithmetic: 18.7 us -> 0 us
  local copies, waits for them, and re-layouts: 23.8 us -> 5.98 us
  between operations: 11.9 us -> 0.67 us
    psum x7 -> x0, blocking collectives: 268 us -> none  [the longest x4 154 us: fit_sum(): return lax.psum(jnp.sum(residual * precond), ('pa', 'pb'))]
    all_to_all x16 -> x0, waiting for transfers between devices: 94.1 us -> none  [the longest x4 24.1 us: precondition(): lax.all_to_all(from_slab(real_part), ('pa', 'pb'), split_axis=0, concat_a...]
    pallas_call x0 -> x1, Pallas kernels: none -> 54.8 us  [on_device(): pl.pallas_call(functools.partial(kernel, na, nb, (nx, ry, rz)), out_shape...]
    all_to_all x16 -> x0, starting transfers between devices: 53.6 us -> none  [the longest x4 22.3 us: precondition(): lax.all_to_all(stacked_real, ('pa', 'pb'), split_axis=0, concat_axis=0, t...]
    ppermute x18 -> x0, waiting for transfers between devices: 27.6 us -> none  [the longest x8 20.4 us: padded_2(): lax.ppermute(lax.slice_in_dim(block, block.shape[dim] - width, None, axis...]
    dot_general x64 -> x0, matrix products: 24.8 us -> none  [apply_along(): jnp.tensordot(matrix, values, axes=([1], [target_dim]), precision=lax.Pre...]
    ppermute x18 -> x0, starting transfers between devices: 17.1 us -> none  [the longest x8 9.65 us: padded_2(): lax.ppermute(lax.slice_in_dim(block, block.shape[dim] - width, None, axis...]
    unnamed x40 -> x8, local copies, waits for them, and re-layouts: 15.2 us -> 0.02 us
  transfers between devices with their start and end apart: 34 -> 0, of which waited for: 31 -> 0; matrix products, arithmetic and copies ran while one was open for 6% -> 0% of each run, Pallas kernels for 0% -> 0%
where the time goes in v1:
time: 61.7 us; the launch traced here: 61.5 us
  Pallas kernels  54.8 us (89%)
  local copies, waits for them, and re-layouts  5.98 us (10%)
  between operations  0.67 us (1%)
    pallas_call x1, Pallas kernels, on_device(): pl.pallas_call(functools.partial(kernel, na, nb, (nx, ry, rz)), out_shape...  54.8 us
    reshape x4, local copies, waits for them, and re-layouts, on_device(): flat = [v.reshape(nx, cells) for v in (right_side, coef_x, coef_y, coef_z)]  3.69 us
    pallas_call x2, local copies, waits for them, and re-layouts, on_device(): pl.pallas_call(functools.partial(kernel, na, nb, (nx, ry, rz)), out_shape...  2.27 us

profile of v1, /device:TPU:0, one launch (start us, length us, event | category | flops | bytes accessed | tf_op | source)
XLA Modules:
  0.0 61.5 jit_solution(546112892669296887)
XLA Ops:
  0.6 0.0 copy-start
  0.6 0.0 copy-start.1
  0.6 1.6 %copy.20.right_ref = f32[32,256]{1,0:T(8,128)} copy(f32[32,256]{0,1:T(8,128)} %bitcast.6) | data formatting | bytes 65536 | tf_op jit(solution)/shard_map/reshape | solution.py:348
  2.3 0.0 copy-done
  2.3 0.0 copy-start.2
  2.3 0.7 %copy.21.cx_ref = f32[32,256]{1,0:T(8,128)} copy(f32[32,256]{0,1:T(8,128)S(1)} %bitcast.7) | data formatting | bytes 65536 | tf_op jit(solution)/shard_map/reshape | solution.py:348
  3.0 0.0 copy-done.1
  3.0 0.7 %copy.22.cy_ref = f32[32,256]{1,0:T(8,128)} copy(f32[32,256]{0,1:T(8,128)S(1)} %bitcast.8) | data formatting | bytes 65536 | tf_op jit(solution)/shard_map/reshape | solution.py:348
  3.7 0.0 copy-done.2
  3.7 0.7 %copy.23.cz_ref = f32[32,256]{1,0:T(8,128)} copy(f32[32,256]{0,1:T(8,128)S(1)} %bitcast.9) | data formatting | bytes 65536 | tf_op jit(solution)/shard_map/reshape | solution.py:348
  4.4 54.8 %shard_map.131 = (f32[32,256]{1,0:T(8,128)}, f32[32,256]{1,0:T(8,128)}) custom-call(f32[32,256]{1,0:T(8,128)} %copy.20.right_ref, f32[32,256]{1,0:T(8,128)} %copy.21.cx_ref, f32[32,256]{1,0:T(8,128)} %copy.22.cy_ref, f32[32,256]{1,0:T(8,128)} %copy.23.cz_ref, bf16[32,96]{1,0:T(8,128)(2,1)} %constant.16.clone.x_fwd, bf16[32,96]{1,0:T(8,128)(2,1)} %constant.17.clone.x_inv, ...), custom_call_target="tpu_custom_call" | custom-call | tf_op jit(solution)/shard_map/pallas_call | solution.py:352
  59.2 0.0 copy-start.3
  59.2 1.5 %copy.24 = f32[32,256]{0,1:T(8,128)} copy(f32[32,256]{1,0:T(8,128)} %get-tuple-element.4) | data formatting | bytes 65536 | tf_op jit(solution)/shard_map/pallas_call | solution.py:352
  60.7 0.0 copy-done.3
  60.7 0.8 %copy.25 = f32[32,256]{0,1:T(8,128)} copy(f32[32,256]{1,0:T(8,128)S(1)} %copy-done.3) | data formatting | bytes 65536 | tf_op jit(solution)/shard_map/pallas_call | solution.py:352
Async XLA Ops:
  0.6 1.7 %copy-start = (f32[32,16,16]{0,2,1:T(8,128)S(1)}, f32[32,16,16]{0,2,1:T(8,128)}, u32[]{:S(2)}) copy-start(f32[32,16,16]{0,2,1:T(8,128)} %param.13) | copy-start | bytes 98308
  0.6 2.3 %copy-start.1 = (f32[32,16,16]{0,2,1:T(8,128)S(1)}, f32[32,16,16]{0,2,1:T(8,128)}, u32[]{:S(2)}) copy-start(f32[32,16,16]{0,2,1:T(8,128)} %param.14) | copy-start | bytes 98308
  2.3 1.4 %copy-start.2 = (f32[32,16,16]{0,2,1:T(8,128)S(1)}, f32[32,16,16]{0,2,1:T(8,128)}, u32[]{:S(2)}) copy-start(f32[32,16,16]{0,2,1:T(8,128)} %param.15) | copy-start | bytes 98308
  59.2 1.5 %copy-start.3 = (f32[32,256]{1,0:T(8,128)S(1)}, f32[32,256]{1,0:T(8,128)}, u32[]{:S(2)}) copy-start(f32[32,256]{1,0:T(8,128)} %get-tuple-element.5) | copy-start | bytes 98308
